TPU v7x, 256 devices: a whole 4x4x8 slice. The times are simulated.
256 devices in a mesh: span: 64 (over y, x, z_lo, core), head: 4 (over z_hi).
Axes of the slice: x: 4, y: 4, z: 8 (z_hi: 4, z_lo: 2; z = z_hi * 2 + z_lo), core: 2. Of those that a mesh axis runs over, the one named last changes fastest.
Arguments:
- decoder_states: bfloat16 [131072, 1024], P('span'), may hold values from -21 to 21
- encodings: bfloat16 [4096, 128, 1024], P('span', 'head'), may hold values from -21 to 21
- neighbor_table: int32 [2048, 2, 2], P('span'), may hold values from 0 to 63, as said below
- query_weight: bfloat16 [1024, 1024], P(None, 'head'), may hold values from -0.1875 to 0.1875
- key_weight: bfloat16 [1024, 1024], P(None, 'head'), may hold values from -0.1875 to 0.1875
- value_weight: bfloat16 [1024, 1024], P(None, 'head'), may hold values from -0.1875 to 0.1875
- out_weight: bfloat16 [1024, 1024], P('head'), may hold values from -0.1875 to 0.1875
Outputs:
- attended: bfloat16 [131072, 1024], P('span', 'head')
Inputs may be any that keep to these rules, and one draw needn't show every extreme that they name: neighbor_table[c, k, 0] is the database shard and neighbor_table[c, k, 1] the slot in that shard of neighbor k of span c; in each aligned block of 32 spans (the spans of one device along `span`) every shard is named by exactly one neighbor, and every slot of every shard is named exactly once in the whole table.
All inputs are finite; a program needn't handle non-finite values.
Results may differ from a plain program's by a relative error of at most 0.012.
The roundings to bfloat16 on the way count: a program that leaves them out, or rounds other values in their place, can miss the bound.
Values may be sent and summed in bfloat16 or wider, within the bound.
A program may use at most 128 MiB of HBM per device.

v0:
```python
import jax
import jax.numpy as jnp
from jax import lax
from jax.sharding import PartitionSpec as P

HEAD_DIM = 64
SPAN_LEN = 64
SEQ_LEN = 2048


def body(
    decoder_states, encodings, neighbor_table, query_weight, key_weight, value_weight, out_weight
):
    peer_count = lax.axis_size("span")
    column_rows = lax.all_to_all(out_weight, "head", split_axis=1, concat_axis=0, tiled=True)
    shard_ids = neighbor_table[:, :, 0].reshape(-1)
    slot_ids = neighbor_table[:, :, 1].reshape(-1)
    entries = shard_ids.shape[0]
    per_peer = entries // peer_count
    numbering = jnp.arange(entries, dtype=jnp.int32)
    same_before = (shard_ids[:, None] == shard_ids[None, :]) & (
        numbering[None, :] < numbering[:, None]
    )
    ranking = jnp.sum(same_before.astype(jnp.int32), axis=1)
    position = shard_ids * per_peer + ranking
    placed = position[None, :] == numbering[:, None]
    request = jnp.sum(jnp.where(placed, slot_ids[None, :], 0), axis=1)
    wanted = lax.all_to_all(request, "span", split_axis=0, concat_axis=0, tiled=True)
    selected = encodings[wanted]
    model_width = decoder_states.shape[1]
    group_cols = query_weight.shape[1]
    both_weights = jnp.concatenate([key_weight, value_weight], axis=1)
    arrived = lax.all_to_all(selected, "span", split_axis=0, concat_axis=0, tiled=True)
    block_in = lax.all_gather(arrived, "head", axis=1, tiled=True)
    flattened = block_in.reshape(-1, model_width)
    result = jnp.dot(flattened, both_weights, preferred_element_type=jnp.float32).astype(
        jnp.bfloat16
    )
    projected = result.reshape(block_in.shape[0], block_in.shape[1], 2 * group_cols)
    ordered = projected[position]
    span_count = neighbor_table.shape[0]
    neighbors = neighbor_table.shape[1]
    heads_here = group_cols // HEAD_DIM
    ordered = ordered.reshape(span_count, neighbors * projected.shape[1], 2 * group_cols)
    key_rows = ordered[:, :, :group_cols].reshape(span_count, -1, heads_here, HEAD_DIM)
    value_rows = ordered[:, :, group_cols:].reshape(span_count, -1, heads_here, HEAD_DIM)
    queries = jnp.dot(decoder_states, query_weight, preferred_element_type=jnp.float32).astype(
        jnp.bfloat16
    )
    sequences = decoder_states.shape[0] // SEQ_LEN
    offset = SPAN_LEN - 1
    queries = queries.reshape(sequences, SEQ_LEN, group_cols)
    shifted = jnp.concatenate(
        [queries[:, offset:], jnp.zeros((sequences, offset, group_cols), jnp.bfloat16)], axis=1
    )
    shifted = shifted.reshape(span_count, SPAN_LEN, heads_here, HEAD_DIM)
    inv_root = HEAD_DIM ** (-0.5)
    scores = (
        jnp.einsum("cqhd,ckhd->chqk", shifted, key_rows, preferred_element_type=jnp.float32)
        * inv_root
    )
    weights = jax.nn.softmax(scores, axis=-1).astype(jnp.bfloat16)
    context = jnp.einsum(
        "chqk,ckhd->cqhd", weights, value_rows, preferred_element_type=jnp.float32
    ).astype(jnp.bfloat16)
    context = context.reshape(sequences, SEQ_LEN, group_cols)
    context = jnp.concatenate(
        [jnp.zeros((sequences, offset, group_cols), jnp.bfloat16), context[:, : SEQ_LEN - offset]],
        axis=1,
    )
    context = context.reshape(-1, group_cols)
    summed = jnp.dot(
        lax.all_gather(context, "head", axis=1, tiled=True),
        column_rows,
        preferred_element_type=jnp.float32,
    )
    return summed.astype(jnp.bfloat16)


def solution(mesh):
    return jax.shard_map(
        body,
        mesh=mesh,
        in_specs=(
            P("span", None),
            P("span", "head", None),
            P("span", None, None),
            P(None, "head"),
            P(None, "head"),
            P(None, "head"),
            P("head", None),
        ),
        out_specs=P("span", "head"),
        check_vma=False,
    )
```

profile of v0, /device:TPU:33, one launch (start us, length us, event | category | flops | bytes accessed | tf_op | source)
XLA Modules:
  0.0 560.3 jit_solution(16839109739039627777)
XLA Ops:
  6.5 0.0 copy-start
  6.5 0.0 all-gather.4.cloned.1.call-start
  6.5 0.8 fusion.30
  7.3 0.1 copy.50
  7.4 0.1 reshape_squeeze.5
  7.5 0.2 convert_reduce_fusion
  7.7 0.1 copy.51
  7.8 0.1 broadcast_in_dim.14
  7.9 0.1 select_reduce_fusion
  8.0 0.1 copy.52
  8.1 15.8 %all_to_all.36 = s32[64,1,1]{2,1,0:T(1,128)S(1)} all-to-all(s32[64,1,1]{2,1,0:T(1,128)S(1)} %copy.52), channel_id=1, replica_groups=mesh['span'=64,'head'=4] {'span'}, dimensions={0} | all-to-all | bytes 512 | tf_op jit(solution)/shard_map/all_to_all | solution.py:28
  23.9 1.2 reduce
  25.1 4.9 gather_fusion
  30.1 56.3 %all_to_all.37 = bf16[64,32,1024]{2,1,0:T(8,128)(2,1)} all-to-all(bf16[64,32,1024]{2,1,0:T(8,128)(2,1)} %gather_fusion), channel_id=1, replica_groups=mesh['span'=64,'head'=4] {'span'}, dimensions={0} | all-to-all | bytes 8388608 | tf_op jit(solution)/shard_map/all_to_all | solution.py:33
  86.4 0.0 all-gather.4.cloned.1.call-update
  86.4 0.2 all-gather.6.cloned.1.call-start
  86.6 0.1 reshape_squeeze.6
  86.7 0.0 copy-done
  86.7 3.4 fusion.11
  90.2 0.0 copy-start.4
  90.2 0.2 slice.29
  90.4 1.0 concatenate.10
  91.5 3.3 reshape.100
  94.8 285.4 %all-gather.4.cloned.1.call-done = bf16[64,128,1024]{2,1,0:T(8,128)(2,1)} async-done(((bf16[64,32,1024]{2,1,0:T(8,128)(2,1)}), bf16[64,128,1024]{2,1,0:T(8,128)(2,1)}) %all-gather.4.cloned.1.call-update) | async-done | bytes 16777232 | tf_op jit(solution)/shard_map/all_gather | solution.py:34
  380.3 0.0 copy-done.4
  380.3 14.5 %convolution_convert_fusion = bf16[8192,512]{1,0:T(8,128)(2,1)} fusion(bf16[8192,1024]{1,0:T(8,128)(2,1)} %bitcast.54, bf16[1024,256]{1,0:T(8,128)(2,1)S(1)} %copy-done.4, bf16[1024,256]{1,0:T(8,128)(2,1)} %param.11), kind=kOutput, calls=%fused_computation.3 | convolution fusion | flops 8596226048 | bytes 26214400 | tf_op jit(solution)/shard_map/dot_general | solution.py:36
  394.8 8.9 %gather_fusion.1 = bf16[64,128,512]{2,1,0:T(8,128)(2,1)} fusion(bf16[64,128,512]{2,1,0:T(8,128)(2,1)} %bitcast.47, s32[1024]{0:T(1024)S(1)} %pad_clamp_fusion), kind=kCustom, calls=%fused_computation.1 | custom fusion | bytes 16777472 | tf_op jit(solution)/shard_map/gather | solution.py:40
  403.7 5.9 %fusion.29 = (bf16[32,256,256]{2,1,0:T(8,128)(2,1)}, bf16[32,256,256]{2,1,0:T(8,128)(2,1)}) fusion(bf16[32,256,512]{2,1,0:T(8,128)(2,1)} %bitcast.45), kind=kLoop, calls=%fused_computation.37 | loop fusion | bytes 16777216 | tf_op jit(solution)/shard_map/slice | solution.py:45
  409.6 6.4 %copy.61 = bf16[32,256,256]{1,2,0:T(8,128)(2,1)} copy(bf16[32,256,256]{2,1,0:T(8,128)(2,1)} %get-tuple-element.5) | data formatting | bytes 8388608
  416.0 3.4 fusion.12
  419.4 0.0 copy-start.2
  419.4 3.1 fusion.31
  422.6 0.1 copy-done.2
  422.6 6.4 %copy.60 = bf16[32,256,256]{1,2,0:T(8,128)(2,1)} copy(bf16[32,256,256]{2,1,0:T(8,128)(2,1)} %get-tuple-element.6) | data formatting | bytes 8388608
  429.0 22.4 %convert_bitcast_fusion = bf16[32,64,4,64]{1,3,2,0:T(8,128)(2,1)} fusion(bf16[32,256,4,64]{1,3,2,0:T(8,128)(2,1)} %bitcast.49, f32[32,4,64]{2,1,0:T(4,128)S(1)} %fusion.31, f32[32,4,64,256]{3,2,1,0:T(8,128)} %copy-done.2), kind=kOutput, calls=%fused_computation.17 | convolution fusion | flops 279453952 | bytes 13664256 | tf_op jit(solution)/shard_map/chqk,ckhd->cqhd/dot_general | solution.py:63
  451.4 2.9 copy.57
  454.4 0.0 copy-start.3
  454.4 2.4 reshape.102
  456.8 2.6 concatenate.11
  459.4 0.0 all-gather.6.cloned.1.call-update
  459.5 0.0 copy-done.3
  459.5 0.2 copy.58
  459.7 16.1 %all_to_all.38 = bf16[256,4,256]{0,2,1:T(8,128)(2,1)S(1)} all-to-all(bf16[256,4,256]{0,2,1:T(8,128)(2,1)S(1)} %bitcast.51), channel_id=1, replica_groups=mesh['span'=64,'head'=4] {'head'}, dimensions={1} | all-to-all | bytes 1048576 | tf_op jit(solution)/shard_map/all_to_all | solution.py:15
  475.8 0.2 copy.59
  476.0 72.9 %all-gather.6.cloned.1.call-done = bf16[1,2048,1024]{1,2,0:T(8,128)(2,1)} async-done(((bf16[1,2048,256]{1,2,0:T(8,128)(2,1)}), bf16[1,2048,1024]{1,2,0:T(8,128)(2,1)}) %all-gather.6.cloned.1.call-update) | async-done | bytes 4194320 | tf_op jit(solution)/shard_map/all_gather | solution.py:73
  548.9 0.0 copy-start.1
  548.9 4.5 fusion.8
  553.4 0.0 copy-done.1
  (5 shorter events, 0.0 us)
Async XLA Ops:
  6.5 80.2 %copy-start = (bf16[1024,256]{1,0:T(8,128)(2,1)S(1)}, bf16[1024,256]{1,0:T(8,128)(2,1)}, u32[]{:S(2)}) copy-start(bf16[1024,256]{1,0:T(8,128)(2,1)} %param.10) | copy-start | bytes 1572868
  6.5 373.7 %all-gather.4.cloned.1.call-start = ((), (), s32[]{:S(2)}) async-start(), calls=%async_computation.3 | async-start | bytes 20971520 | tf_op jit(solution)/shard_map/all_gather | solution.py:34
  86.4 462.5 %all-gather.6.cloned.1.call-start = ((), (), s32[]{:S(2)}) async-start(), calls=%async_computation.4 | async-start | bytes 5242880 | tf_op jit(solution)/shard_map/all_gather | solution.py:73
  90.2 290.1 %copy-start.4 = (bf16[1024,256]{1,0:T(8,128)(2,1)S(1)}, bf16[1024,256]{1,0:T(8,128)(2,1)}, u32[]{:S(2)}) copy-start(bf16[1024,256]{1,0:T(8,128)(2,1)} %param.12) | copy-start | bytes 1572868
  419.4 3.2 copy-start.2
  454.4 5.1 copy-start.3
  548.9 4.6 copy-start.1
Sparse Core Ops, SparseCore 0:
  86.5 293.6 all-gather.3
  459.6 89.2 all-gather.5
where the time goes:
time: 561 us; the launch traced here: 560 us
  waiting for transfers between devices  358 us (64%)
  blocking collectives  88.2 us (16%)
  matrix products  48.3 us (9%)
  local copies, waits for them, and re-layouts  47 us (8%)
  between operations  13.5 us (2%)
    all_gather x1, waiting for transfers between devices, body(): block_in = lax.all_gather(arrived, 'head', axis=1, tiled=True)  285 us
    all_gather x1, waiting for transfers between devices, body(): lax.all_gather(context, 'head', axis=1, tiled=True)  72.9 us
    all_to_all x1, blocking collectives, body(): lax.all_to_all(selected, 'span', split_axis=0, concat_axis=0, tiled=True)  56.3 us
    dot_general x1, matrix products, body(): jnp.einsum('chqk,ckhd->cqhd', weights, value_rows, preferred_element_type...  22.4 us
    all_to_all x1, blocking collectives, body(): lax.all_to_all(out_weight, 'head', split_axis=1, concat_axis=0, tiled=True)  16.1 us
    all_to_all x1, blocking collectives, body(): lax.all_to_all(request, 'span', split_axis=0, concat_axis=0, tiled=True)  15.8 us
    dot_general x1, matrix products, body(): jnp.dot(flattened, both_weights, preferred_element_type=jnp.float32)  14.5 us
    unnamed x13, local copies, waits for them, and re-layouts  13.1 us
  transfers between devices with their start and end apart: 2, of which 2 were waited for; matrix products, arithmetic and copies ran while one was open for 2% of the time, Pallas kernels for 0%

commit v1 on v0

--- a/solution.py
+++ b/solution.py
@@ -70,7 +70,9 @@
     )
     context = context.reshape(-1, group_cols)
     summed = jnp.dot(
-        lax.all_gather(context, "head", axis=1, tiled=True),
+        jnp.concatenate(
+            lax.all_to_all(jnp.stack([context] * lax.axis_size("head")), "head", 0, 0), axis=1
+        ),
         column_rows,
         preferred_element_type=jnp.float32,
     )

time: 561 us -> 571 us (1.018)
  the two profiles are of different devices: /device:TPU:33 before, /device:TPU:26 now
where the time goes in v1:
time: 571 us; the launch traced here: 570 us
  blocking collectives  250 us (44%)
  waiting for transfers between devices  199 us (35%)
  local copies, waits for them, and re-layouts  48.8 us (9%)
  matrix products  46.1 us (8%)
  between operations  13.5 us (2%)
  starting transfers between devices  7.56 us (1%)
    all_gather x1, waiting for transfers between devices, body(): block_in = lax.all_gather(arrived, 'head', axis=1, tiled=True)  199 us
    all_to_all x1, blocking collectives, body(): lax.all_to_all(jnp.stack([context] * lax.axis_size('head')), 'head', 0, 0)  179 us
    all_to_all x1, blocking collectives, body(): lax.all_to_all(selected, 'span', split_axis=0, concat_axis=0, tiled=True)  57.1 us
    dot_general x1, matrix products, body(): jnp.einsum('chqk,ckhd->cqhd', weights, value_rows, preferred_element_type...  22.4 us
    dot_general x1, matrix products, body(): jnp.dot(flattened, both_weights, preferred_element_type=jnp.float32)  14.6 us
    all_to_all x1, blocking collectives, body(): lax.all_to_all(request, 'span', split_axis=0, concat_axis=0, tiled=True)  14.2 us
    unnamed x11, local copies, waits for them, and re-layouts  14.1 us
  transfers between devices with their start and end apart: 2, of which 1 were waited for; matrix products, arithmetic and copies ran while one was open for 15% of the time, Pallas kernels for 0%

profile of v1, /device:TPU:26, one launch (start us, length us, event | category | flops | bytes accessed | tf_op | source)
XLA Modules:
  0.0 570.0 jit_solution(7651532307363425438)
XLA Ops:
  6.5 0.0 copy-start
  6.5 0.0 all-gather.2.cloned.1.call-start
  6.5 0.8 fusion.34
  7.3 0.1 copy.46
  7.4 0.1 reshape_squeeze.5
  7.5 0.2 convert_reduce_fusion
  7.7 0.1 copy.47
  7.8 0.1 broadcast_in_dim.14
  7.9 0.1 select_reduce_fusion
  8.0 0.1 copy.48
  8.1 14.2 %all_to_all.38 = s32[64,1,1]{2,1,0:T(1,128)S(1)} all-to-all(s32[64,1,1]{2,1,0:T(1,128)S(1)} %copy.48), channel_id=1, replica_groups=mesh['span'=64,'head'=4] {'span'}, dimensions={0} | all-to-all | bytes 512 | tf_op jit(solution)/shard_map/all_to_all | solution.py:28
  22.3 1.2 reduce
  23.5 4.9 gather_fusion
  28.5 57.1 %all_to_all.39 = bf16[64,32,1024]{2,1,0:T(8,128)(2,1)} all-to-all(bf16[64,32,1024]{2,1,0:T(8,128)(2,1)} %gather_fusion), channel_id=1, replica_groups=mesh['span'=64,'head'=4] {'span'}, dimensions={0} | all-to-all | bytes 8388608 | tf_op jit(solution)/shard_map/all_to_all | solution.py:33
  85.6 0.0 copy-start.3
  85.6 0.0 all-gather.2.cloned.1.call-update
  85.6 1.0 copy-done.3
  86.6 0.2 copy.55
  86.8 1.1 copy.56
  87.9 7.6 %all-to-all-start.3 = ((bf16[256,4,256]{2,0,1:T(8,128)(2,1)}), bf16[256,4,256]{2,0,1:T(8,128)(2,1)S(1)}, u32[]{:S(2)}, u32[]{:S(2)}) async-start(bf16[256,4,256]{2,0,1:T(8,128)(2,1)} %copy.56), calls=%async_computation.3 | async-start | bytes 1048576 | tf_op jit(solution)/shard_map/all_to_all | solution.py:15
  95.5 0.1 reshape_squeeze.6
  95.6 0.0 copy-done
  95.6 3.4 fusion.14
  99.0 0.2 slice.29
  99.3 1.0 concatenate.12
  100.3 3.4 reshape.102
  103.8 199.0 %all-gather.2.cloned.1.call-done = bf16[64,128,1024]{2,1,0:T(8,128)(2,1)} async-done(((bf16[64,32,1024]{2,1,0:T(8,128)(2,1)}), bf16[64,128,1024]{2,1,0:T(8,128)(2,1)}) %all-gather.2.cloned.1.call-update) | async-done | bytes 16777232 | tf_op jit(solution)/shard_map/all_gather | solution.py:34
  302.8 14.6 %convolution_convert_fusion = bf16[8192,512]{1,0:T(8,128)(2,1)} fusion(bf16[8192,1024]{1,0:T(8,128)(2,1)} %bitcast.60, bf16[1024,256]{1,0:T(8,128)(2,1)} %param.12, bf16[1024,256]{1,0:T(8,128)(2,1)} %param.11), kind=kOutput, calls=%fused_computation.3 | convolution fusion | flops 8596226048 | bytes 26214400 | tf_op jit(solution)/shard_map/dot_general | solution.py:36
  317.4 8.9 %gather_fusion.1 = bf16[64,128,512]{2,1,0:T(8,128)(2,1)} fusion(bf16[64,128,512]{2,1,0:T(8,128)(2,1)} %bitcast.55, s32[1024]{0:T(1024)S(1)} %pad_clamp_fusion), kind=kCustom, calls=%fused_computation.1 | custom fusion | bytes 16777472 | tf_op jit(solution)/shard_map/gather | solution.py:40
  326.4 5.9 %fusion.33 = (bf16[32,256,256]{2,1,0:T(8,128)(2,1)}, bf16[32,256,256]{2,1,0:T(8,128)(2,1)}) fusion(bf16[32,256,512]{2,1,0:T(8,128)(2,1)} %bitcast.53), kind=kLoop, calls=%fused_computation.40 | loop fusion | bytes 16777216 | tf_op jit(solution)/shard_map/slice | solution.py:45
  332.3 6.4 %copy.58 = bf16[32,256,256]{1,2,0:T(8,128)(2,1)} copy(bf16[32,256,256]{2,1,0:T(8,128)(2,1)} %get-tuple-element.5) | data formatting | bytes 8388608
  338.7 3.4 fusion.15
  342.1 0.0 copy-start.2
  342.1 3.1 fusion.35
  345.2 0.1 copy-done.2
  345.3 6.4 %copy.57 = bf16[32,256,256]{1,2,0:T(8,128)(2,1)} copy(bf16[32,256,256]{2,1,0:T(8,128)(2,1)} %get-tuple-element.6) | data formatting | bytes 8388608
  351.7 22.4 %convert_bitcast_fusion = bf16[32,64,4,64]{1,3,2,0:T(8,128)(2,1)} fusion(bf16[32,256,4,64]{1,3,2,0:T(8,128)(2,1)} %bitcast.57, f32[32,4,64]{2,1,0:T(4,128)S(1)} %fusion.35, f32[32,4,64,256]{3,2,1,0:T(8,128)} %copy-done.2), kind=kOutput, calls=%fused_computation.18 | convolution fusion | flops 279453952 | bytes 13664256 | tf_op jit(solution)/shard_map/chqk,ckhd->cqhd/dot_general | solution.py:63
  374.1 2.9 copy.53
  377.0 2.4 reshape.104
  379.5 1.6 pad_bitcast_fusion
  381.1 0.5 copy.54
  381.6 0.0 all-to-all-done.3
  381.7 0.3 stack.3
  381.9 0.0 copy-start.1
  381.9 179.0 %all_to_all.40 = bf16[4,2048,256]{2,1,0:T(8,128)(2,1)S(1)} all-to-all(bf16[4,2048,256]{2,1,0:T(8,128)(2,1)S(1)} %stack.3), channel_id=1, replica_groups=mesh['span'=64,'head'=4] {'head'}, dimensions={0} | all-to-all | bytes 8388608 | tf_op jit(solution)/shard_map/all_to_all | solution.py:74
  561.0 2.2 fusion.11
  563.2 0.0 copy-done.1
  (5 shorter events, 0.0 us)
Async XLA Ops:
  6.5 89.0 %copy-start = (bf16[1024,256]{1,0:T(8,128)(2,1)S(1)}, bf16[1024,256]{1,0:T(8,128)(2,1)}, u32[]{:S(2)}) copy-start(bf16[1024,256]{1,0:T(8,128)(2,1)} %param.10) | copy-start | bytes 1572868
  6.5 296.3 %all-gather.2.cloned.1.call-start = ((), (), s32[]{:S(2)}) async-start(), calls=%async_computation.4 | async-start | bytes 20971520 | tf_op jit(solution)/shard_map/all_gather | solution.py:34
  85.6 1.0 copy-start.3
  87.9 293.8 %all-to-all-start.3 = ((bf16[256,4,256]{2,0,1:T(8,128)(2,1)}), bf16[256,4,256]{2,0,1:T(8,128)(2,1)S(1)}, u32[]{:S(2)}, u32[]{:S(2)}) async-start(bf16[256,4,256]{2,0,1:T(8,128)(2,1)} %copy.56), calls=%async_computation.3 | async-start | bytes 1048576 | tf_op jit(solution)/shard_map/all_to_all | solution.py:15
  342.1 3.2 copy-start.2
  381.9 181.3 %copy-start.1 = (bf16[1024,256]{1,0:T(8,128)(2,1)S(1)}, bf16[1024,256]{1,0:T(8,128)(2,1)}, u32[]{:S(2)}) copy-start(bf16[1024,256]{1,0:T(8,128)(2,1)} %param.10) | copy-start | bytes 1572868
Sparse Core Ops, SparseCore 0:
  85.7 217.0 all-gather.1
